TPU v7x, 32 devices: a whole 2x2x4 slice. The times are simulated.
32 devices in a mesh: ep: 4 (over y, core), fsdp: 8 (over z, x).
Axes of the slice: x: 2, y: 2, z: 4, core: 2. Of those that a mesh axis runs over, the one named last changes fastest.
Arguments:
- master_down: float32 [16, 6400, 4096], P('ep', None, 'fsdp'), may hold values from -0.109375 to 0.109375
- second_down: bfloat16 [16, 6400, 4096], P('ep', None, 'fsdp'), may hold values from -0.0390625 to 0.0390625
- router_weight: float32 [4096, 16], P('fsdp', 'ep'), may hold values from -0.09375 to 0.09375
- router_gain: float32 [4096], P('fsdp'), may hold values from 0.25 to 1.75
Outputs:
- final_down: bfloat16 [16, 6400, 4096], P('ep', 'fsdp')
- scale_down: float32 [16, 6400], P('ep', 'fsdp')
- serve_router: bfloat16 [4096, 16], replicated
All inputs are finite; a program needn't handle non-finite values.
Results may differ from a plain program's by a relative error of at most 0.001.
Values may be sent and summed in bfloat16 or wider, within the bound.
A program may use at most 256 MiB of HBM per device.

v0:
```python
import jax
import jax.numpy as jnp
from jax import lax
from jax.sharding import PartitionSpec as P


def shards(master_down, second_down, router_weight, router_gain):
    merged_down = master_down + second_down.astype(jnp.float32)
    total_down = lax.psum(jnp.sum(merged_down * merged_down, axis=2), "fsdp")
    scale_down = jnp.sqrt(total_down)
    narrow_down = (merged_down / jnp.expand_dims(scale_down, 2)).astype(jnp.bfloat16)
    final_down = lax.all_to_all(narrow_down, "fsdp", split_axis=1, concat_axis=2, tiled=True)
    scale_down = lax.dynamic_slice_in_dim(
        scale_down, lax.axis_index("fsdp") * final_down.shape[1], final_down.shape[1], axis=1
    )
    part_router = (router_weight * router_gain[:, None]).astype(jnp.bfloat16)
    row_router = lax.all_gather(part_router, "fsdp", axis=0, tiled=True)
    serve_router = lax.all_gather(row_router, "ep", axis=1, tiled=True)
    return (final_down, scale_down, serve_router)


def solution(mesh):
    return jax.shard_map(
        shards,
        mesh=mesh,
        in_specs=(P("ep", None, "fsdp"), P("ep", None, "fsdp"), P("fsdp", "ep"), P("fsdp")),
        out_specs=(P("ep", "fsdp", None), P("ep", "fsdp"), P()),
        check_vma=False,
    )
```

profile of v0, /device:TPU:0, one launch (start us, length us, event | category | flops | bytes accessed | tf_op | source)
XLA Modules:
  0.0 905.5 jit_solution(8188198296431997854)
XLA Ops:
  7.2 0.0 all-reduce.2.cloned.1.call-start
  7.2 24.2 %multiply_reduce_fusion = f32[4,6400]{1,0:T(4,128)S(1)} fusion(f32[4,6400,512]{2,1,0:T(8,128)} %param.4, bf16[4,6400,512]{2,1,0:T(8,128)(2,1)} %param.5), kind=kLoop, calls=%fused_computation.1 | loop fusion | flops 52403200 | bytes 78745600 | tf_op jit(solution)/shard_map/reduce_sum | solution.py:9
  31.4 2.3 copy.21
  33.7 0.0 all-reduce.2.cloned.1.call-update
  33.7 135.6 %all-reduce.2.cloned.1.call-done = f32[4,6400]{0,1:T(8,128)} async-done(((f32[4,6400]{0,1:T(8,128)}), f32[4,6400]{0,1:T(8,128)}) %all-reduce.2.cloned.1.call-update) | async-done | bytes 102416 | tf_op jit(solution)/shard_map/psum | solution.py:9
  169.3 2.7 sqrt.3
  172.0 1.2 copy.17
  173.3 34.3 %divide_convert_fusion = bf16[4,6400,512]{2,1,0:T(8,128)(2,1)} fusion(f32[4,6400,512]{2,1,0:T(8,128)} %param.4, bf16[4,6400,512]{2,1,0:T(8,128)(2,1)} %param.5, f32[4,6400]{1,0:T(4,128)S(1)} %copy.17), kind=kLoop, calls=%fused_computation | loop fusion | flops 52428800 | bytes 104960000 | tf_op jit(solution)/shard_map/convert_element_type | solution.py:11
  207.5 33.4 %copy.18 = bf16[4,6400,512]{2,0,1:T(4,128)(2,1)} copy(bf16[4,6400,512]{2,1,0:T(8,128)(2,1)} %divide_convert_fusion) | data formatting | bytes 52428800 | tf_op jit(solution)/shard_map/convert_element_type | solution.py:11
  240.9 0.0 copy-start
  240.9 0.0 copy-start.1
  240.9 6.6 all-to-all-start
  247.6 0.0 copy-done
  247.6 0.0 copy-done.1
  247.6 585.0 %all_gather.6 = bf16[4096,4]{0,1:T(4,128)(2,1)S(1)} all-gather(bf16[512,4]{0,1:T(4,128)(2,1)S(1)} %multiply_convert_fusion), channel_id=1, replica_groups=mesh['ep'=4,'fsdp'=8] {'fsdp'}, dimensions={0}, use_global_device_ids=true | all-gather | bytes 36864 | tf_op jit(solution)/shard_map/all_gather | solution.py:17
  832.7 5.4 all-gather
  838.1 0.7 reshape.9
  838.8 0.8 constant_dynamic-slice_fusion
  839.5 1.8 copy.20
  841.3 0.0 all-to-all-done
  841.3 18.2 %copy.19 = bf16[4,800,8,512]{3,2,1,0:T(8,128)(2,1)} copy(bf16[4,800,8,512]{3,0,1,2:T(4,128)(2,1)} %bitcast.1) | data formatting | bytes 52428800 | tf_op jit(solution)/shard_map/all_to_all | solution.py:12
  859.5 39.2 %all_to_all.16 = bf16[4,800,4096]{2,1,0:T(8,128)(2,1)} reshape(bf16[4,800,8,512]{3,2,1,0:T(8,128)(2,1)} %copy.19) | data formatting | bytes 52428800 | tf_op jit(solution)/shard_map/all_to_all | solution.py:12
  (1 shorter events, 0.0 us)
Async XLA Ops:
  7.2 162.2 %all-reduce.2.cloned.1.call-start = ((), (), s32[]{:S(2)}) async-start(), calls=%async_computation.1 | async-start | bytes 6553600 | tf_op jit(solution)/shard_map/psum | solution.py:9
  240.9 6.7 copy-start
  240.9 6.7 copy-start.1
  240.9 600.4 %all-to-all-start = ((bf16[4,6400,512]{2,0,1:T(4,128)(2,1)}), bf16[4,6400,512]{2,0,1:T(4,128)(2,1)}, u32[]{:S(2)}, u32[]{:S(2)}) async-start(bf16[4,6400,512]{2,0,1:T(4,128)(2,1)} %copy.18), calls=%async_computation | async-start | bytes 52428800 | tf_op jit(solution)/shard_map/all_to_all | solution.py:12
Sparse Core Ops, SparseCore 0:
  33.9 135.4 all-reduce.1
where the time goes:
time: 907 us; the launch traced here: 906 us
  blocking collectives  590 us (65%)
  waiting for transfers between devices  136 us (15%)
  local copies, waits for them, and re-layouts  100 us (11%)
  other arithmetic  58.5 us (6%)
  between operations  14.1 us (2%)
    all_gather x1, blocking collectives, shards(): row_router = lax.all_gather(part_router, 'fsdp', axis=0, tiled=True)  585 us
    psum x1, waiting for transfers between devices, shards(): total_down = lax.psum(jnp.sum(merged_down * merged_down, axis=2), 'fsdp')  136 us
    all_to_all x2, local copies, waits for them, and re-layouts, shards(): lax.all_to_all(narrow_down, 'fsdp', split_axis=1, concat_axis=2, tiled=True)  57.4 us
    convert_element_type x1, other arithmetic, shards(): (merged_down / jnp.expand_dims(scale_down, 2)).astype(jnp.bfloat16)  34.3 us
    convert_element_type x1, local copies, waits for them, and re-layouts, shards(): (merged_down / jnp.expand_dims(scale_down, 2)).astype(jnp.bfloat16)  33.4 us
    reduce_sum x1, other arithmetic, shards(): total_down = lax.psum(jnp.sum(merged_down * merged_down, axis=2), 'fsdp')  24.2 us
  transfers between devices with their start and end apart: 2, of which 1 were waited for; matrix products, arithmetic and copies ran while one was open for 0% of the time, Pallas kernels for 0%

commit v1 on v0

--- a/solution.py
+++ b/solution.py
@@ -6,7 +6,7 @@
 
 def shards(master_down, second_down, router_weight, router_gain):
     merged_down = master_down + second_down.astype(jnp.float32)
-    total_down = lax.psum(jnp.sum(merged_down * merged_down, axis=2), "fsdp")
+    total_down = jnp.sum(lax.all_gather(jnp.sum(merged_down * merged_down, axis=2), "fsdp"), axis=0)
     scale_down = jnp.sqrt(total_down)
     narrow_down = (merged_down / jnp.expand_dims(scale_down, 2)).astype(jnp.bfloat16)
     final_down = lax.all_to_all(narrow_down, "fsdp", split_axis=1, concat_axis=2, tiled=True)

time: 907 us -> 781 us (0.86)
  waiting for transfers between devices: 136 us -> 0.01 us
  blocking collectives: 590 us -> 620 us
  between operations: 14.1 us -> 0.71 us
    psum x1 -> x0, waiting for transfers between devices: 136 us -> none  [shards(): total_down = lax.psum(jnp.sum(merged_down * merged_down, axis=2), 'fsdp')]
    all_gather x0 -> x1, blocking collectives: none -> 33.9 us  [shards(): lax.all_gather(jnp.sum(merged_down * merged_down, axis=2), 'fsdp')]
    reduce_sum x1 -> x2, other arithmetic: 24.2 us -> 24.4 us  [the longest x1 24.2 us: shards(): jnp.sum(merged_down * merged_down, axis=2)]
  transfers between devices with their start and end apart: 2 -> 1, of which waited for: 1 -> 0; matrix products, arithmetic and copies ran while one was open for 0% -> 0% of each run, Pallas kernels for 0% -> 0%
where the time goes in v1:
time: 781 us; the launch traced here: 780 us
  blocking collectives  620 us (79%)
  local copies, waits for them, and re-layouts  94.5 us (12%)
  other arithmetic  58.7 us (8%)
    all_gather x1, blocking collectives, shards(): row_router = lax.all_gather(part_router, 'fsdp', axis=0, tiled=True)  580 us
    all_to_all x2, local copies, waits for them, and re-layouts, shards(): lax.all_to_all(narrow_down, 'fsdp', split_axis=1, concat_axis=2, tiled=True)  57.4 us
    convert_element_type x1, other arithmetic, shards(): (merged_down / jnp.expand_dims(scale_down, 2)).astype(jnp.bfloat16)  34.3 us
    all_gather x1, blocking collectives, shards(): lax.all_gather(jnp.sum(merged_down * merged_down, axis=2), 'fsdp')  33.9 us
    convert_element_type x1, local copies, waits for them, and re-layouts, shards(): (merged_down / jnp.expand_dims(scale_down, 2)).astype(jnp.bfloat16)  33.4 us
    reduce_sum x1, other arithmetic, shards(): jnp.sum(merged_down * merged_down, axis=2)  24.2 us
  transfers between devices with their start and end apart: 1, of which 0 were waited for; matrix products, arithmetic and copies ran while one was open for 0% of the time, Pallas kernels for 0%

profile of v1, /device:TPU:0, one launch (start us, length us, event | category | flops | bytes accessed | tf_op | source)
XLA Modules:
  0.0 780.0 jit_solution(1847130021066882002)
XLA Ops:
  0.6 24.2 %multiply_reduce_fusion = f32[4,6400]{1,0:T(4,128)S(1)} fusion(f32[4,6400,512]{2,1,0:T(8,128)} %param.4, bf16[4,6400,512]{2,1,0:T(8,128)(2,1)} %param.5), kind=kLoop, calls=%fused_computation.1 | loop fusion | flops 52403200 | bytes 78745600 | tf_op jit(solution)/shard_map/reduce_sum | solution.py:9
  24.9 1.1 copy.21
  26.0 1.2 copy.18
  27.2 33.9 %all-gather.1 = f32[8,4,6400]{2,1,0:T(4,128)S(1)} all-gather(f32[1,4,6400]{2,1,0:T(4,128)S(1)} %copy.18), channel_id=2, replica_groups=mesh['ep'=4,'fsdp'=8] {'fsdp'}, dimensions={0}, use_global_device_ids=true | all-gather | bytes 921600 | tf_op jit(solution)/shard_map/all_gather | solution.py:9
  61.2 0.1 reduce_sum.19
  61.3 0.1 sqrt.7
  61.4 34.3 %divide_convert_fusion = bf16[4,6400,512]{2,1,0:T(8,128)(2,1)} fusion(f32[4,6400,512]{2,1,0:T(8,128)} %param.4, bf16[4,6400,512]{2,1,0:T(8,128)(2,1)} %param.5, f32[4,6400]{1,0:T(4,128)S(1)} %sqrt.7), kind=kLoop, calls=%fused_computation | loop fusion | flops 52428800 | bytes 104960000 | tf_op jit(solution)/shard_map/convert_element_type | solution.py:11
  95.6 0.0 copy-start
  95.6 0.0 copy-start.1
  95.7 33.4 %copy.19 = bf16[4,6400,512]{2,0,1:T(4,128)(2,1)} copy(bf16[4,6400,512]{2,1,0:T(8,128)(2,1)} %divide_convert_fusion) | data formatting | bytes 52428800 | tf_op jit(solution)/shard_map/convert_element_type | solution.py:11
  129.0 6.5 all-to-all-start
  135.5 0.0 copy-done
  135.6 0.0 copy-done.1
  135.6 580.2 %all_gather.14 = bf16[4096,4]{0,1:T(4,128)(2,1)S(1)} all-gather(bf16[512,4]{0,1:T(4,128)(2,1)S(1)} %multiply_convert_fusion), channel_id=1, replica_groups=mesh['ep'=4,'fsdp'=8] {'fsdp'}, dimensions={0}, use_global_device_ids=true | all-gather | bytes 36864 | tf_op jit(solution)/shard_map/all_gather | solution.py:17
  715.8 5.4 all-gather.2
  721.2 0.7 reshape.14
  721.9 0.7 constant_dynamic-slice_fusion
  722.6 0.0 all-to-all-done
  722.6 18.2 %copy.20 = bf16[4,800,8,512]{3,2,1,0:T(8,128)(2,1)} copy(bf16[4,800,8,512]{3,0,1,2:T(4,128)(2,1)} %bitcast.2) | data formatting | bytes 52428800 | tf_op jit(solution)/shard_map/all_to_all | solution.py:12
  740.8 39.2 %all_to_all.16 = bf16[4,800,4096]{2,1,0:T(8,128)(2,1)} reshape(bf16[4,800,8,512]{3,2,1,0:T(8,128)(2,1)} %copy.20) | data formatting | bytes 52428800 | tf_op jit(solution)/shard_map/all_to_all | solution.py:12
  (1 shorter events, 0.0 us)
Async XLA Ops:
  95.6 39.9 %copy-start = (f32[512,4]{0,1:T(4,128)S(1)}, f32[512,4]{0,1:T(4,128)}, u32[]{:S(2)}) copy-start(f32[512,4]{0,1:T(4,128)} %param.6) | copy-start | bytes 24580
  95.6 39.9 %copy-start.1 = (f32[512]{0:T(512)S(1)}, f32[512]{0:T(512)}, u32[]{:S(2)}) copy-start(f32[512]{0:T(512)} %param.7) | copy-start | bytes 6148
  129.0 593.6 %all-to-all-start = ((bf16[4,6400,512]{2,0,1:T(4,128)(2,1)}), bf16[4,6400,512]{2,0,1:T(4,128)(2,1)}, u32[]{:S(2)}, u32[]{:S(2)}) async-start(bf16[4,6400,512]{2,0,1:T(4,128)(2,1)} %copy.19), calls=%async_computation | async-start | bytes 52428800 | tf_op jit(solution)/shard_map/all_to_all | solution.py:12
